TPU v7x, 32 devices: a whole 2x2x4 slice. The times are simulated.
32 devices in a mesh: sx: 8 (over z, y), sy: 4 (over x, core).
Axes of the slice: x: 2, y: 2, z: 4, core: 2. Of those that a mesh axis runs over, the one named last changes fastest.
Arguments:
- tensors: bfloat16 [2, 8, 4, 1024, 256], P(None, 'sx', 'sy'), may hold values from -6 to 6
- gates: bfloat16 [5, 2, 2, 256, 256], replicated, may hold values from -0.1875 to 0.1875
- closing_rows: bfloat16 [2, 4096, 1024], P(None, ('sx', 'sy')), may hold values from -0.125 to 0.125
- closing_columns: float32 [2, 4096, 256], P(None, ('sx', 'sy')), may hold values from -0.25 to 0.25
Outputs:
- amplitudes: float32 [2, 4096], replicated
All inputs are finite; a program needn't handle non-finite values.
Results may differ from a plain program's by a relative error of at most 0.012.
Values may be sent and summed in bfloat16 or wider, within the bound.
A program may use at most 64 MiB of HBM per device.

v0:
```python
import jax
import jax.numpy as jnp
from jax import lax
from jax.sharding import PartitionSpec as P


def mixing_matrix(gate_pair, sign):
    own_top = jnp.concatenate([gate_pair[0, 0], gate_pair[0, 1]], axis=1)
    own_low = jnp.concatenate([-gate_pair[0, 1], gate_pair[0, 0]], axis=1)
    far_top = jnp.concatenate([gate_pair[1, 0], gate_pair[1, 1]], axis=1) * sign
    far_low = jnp.concatenate([-gate_pair[1, 1], gate_pair[1, 0]], axis=1) * sign
    return jnp.concatenate([own_top, own_low, far_top, far_low], axis=0)


def combine(own, partner, matrix):
    width = own.shape[-1]
    leading = own.shape[1:-1]
    joined = jnp.concatenate([own[0], own[1], partner[0], partner[1]], axis=-1).reshape(
        -1, 4 * width
    )
    result = jnp.dot(joined, matrix, preferred_element_type=jnp.float32).astype(jnp.bfloat16)
    real_part = result[:, :width].reshape(leading + (width,))
    imag_part = result[:, width:].reshape(leading + (width,))
    return jnp.stack([real_part, imag_part])


def local_section(grouped, gate_pair, axis_dim, bit_pos):
    shape = grouped.shape
    count = shape[axis_dim]
    split = shape[:axis_dim] + (count >> bit_pos + 1, 2, 1 << bit_pos) + shape[axis_dim + 1 :]
    blocks = grouped.reshape(split)
    lower = lax.index_in_dim(blocks, 0, axis_dim + 1, keepdims=False)
    upper = lax.index_in_dim(blocks, 1, axis_dim + 1, keepdims=False)
    new_lower = combine(lower, upper, mixing_matrix(gate_pair, 1.0))
    new_upper = combine(upper, lower, mixing_matrix(gate_pair, -1.0))
    return jnp.stack([new_lower, new_upper], axis=axis_dim + 1).reshape(shape)


def close_columns(projected, closing_columns):
    amp_real = jnp.sum(
        projected[0] * closing_columns[0] - projected[1] * closing_columns[1], axis=-1
    )
    amp_imag = jnp.sum(
        projected[0] * closing_columns[1] + projected[1] * closing_columns[0], axis=-1
    )
    return jnp.stack([amp_real, amp_imag])


def combine_rows(closing_rows, current):
    proj_real = jnp.dot(closing_rows[0], current[0], preferred_element_type=jnp.float32) - jnp.dot(
        closing_rows[1], current[1], preferred_element_type=jnp.float32
    )
    proj_imag = jnp.dot(closing_rows[0], current[1], preferred_element_type=jnp.float32) + jnp.dot(
        closing_rows[1], current[0], preferred_element_type=jnp.float32
    )
    return jnp.stack([proj_real, proj_imag])


def local(tensors, gates, closing_rows, closing_columns):
    current = tensors[:, 0, 0]
    rows_dev = current.shape[1]
    width = current.shape[2]
    count_x = lax.axis_size("sx")
    count_y = lax.axis_size("sy")
    bits_x = count_x.bit_length() - 1
    bits_y = count_y.bit_length() - 1
    grouped = lax.all_to_all(
        current.reshape(2, count_x, rows_dev // count_x, width),
        "sx",
        split_axis=1,
        concat_axis=1,
        tiled=True,
    )
    for bit_pos in range(bits_x):
        grouped = local_section(grouped, gates[bit_pos], 1, bit_pos)
    current = lax.all_to_all(grouped, "sx", split_axis=1, concat_axis=1, tiled=True).reshape(
        2, rows_dev, width
    )
    grouped = lax.all_to_all(
        current.reshape(2, count_y, rows_dev // count_y, width),
        "sy",
        split_axis=1,
        concat_axis=1,
        tiled=True,
    )
    for bit_pos in range(bits_y):
        grouped = local_section(grouped, gates[bits_x + bit_pos], 1, bit_pos)
    current = lax.all_to_all(grouped, "sy", split_axis=1, concat_axis=1, tiled=True).reshape(
        2, rows_dev, width
    )
    closed = close_columns(combine_rows(closing_rows, current), closing_columns)
    return lax.all_gather(closed, ("sx", "sy"), axis=1, tiled=True)


def solution(mesh):
    placed = (
        P(None, "sx", "sy", None, None),
        P(),
        P(None, ("sx", "sy"), None),
        P(None, ("sx", "sy"), None),
    )
    return jax.shard_map(local, mesh=mesh, in_specs=placed, out_specs=P(), check_vma=False)
```

profile of v0, /device:TPU:0, one launch (start us, length us, event | category | flops | bytes accessed | tf_op | source)
XLA Modules:
  0.0 157.4 jit_solution(10815839486201930402)
XLA Ops:
  0.0 2.3 %copy.47 = bf16[2,8,128,256]{3,2,0,1:T(8,128)(2,1)} copy(bf16[2,8,128,256]{3,2,1,0:T(8,128)(2,1)} %bitcast.207) | data formatting | bytes 2097152 | tf_op jit(solution)/shard_map/reshape;squeeze | solution.py:68
  2.3 7.3 %all-to-all-start = ((bf16[2,8,128,256]{3,2,0,1:T(8,128)(2,1)}), bf16[2,8,128,256]{3,2,0,1:T(8,128)(2,1)S(1)}, u32[]{:S(2)}, u32[]{:S(2)}) async-start(bf16[2,8,128,256]{3,2,0,1:T(8,128)(2,1)} %copy.47), calls=%async_computation | async-start | bytes 2097152 | tf_op jit(solution)/shard_map/all_to_all | solution.py:67
  9.6 1.9 %slice_bitcast_fusion = (bf16[2,2,256,256]{3,2,1,0:T(8,128)(2,1)S(1)}, bf16[2,2,256,256]{3,2,1,0:T(8,128)(2,1)S(1)}, bf16[2,2,256,256]{3,2,1,0:T(8,128)(2,1)S(1)...) fusion(bf16[5,2,2,256,256]{4,3,2,1,0:T(8,128)(2,1)} %param.5), kind=kLoop, calls=%fused_computation.162 | loop fusion | bytes 5242880 | tf_op jit(solution)/shard_map/squeeze | solution.py:87
  11.5 0.7 slice_bitcast_fusion.23
  12.2 0.7 fusion.156
  13.0 0.9 maximum_multiply_fusion
  13.9 0.8 slice_bitcast_fusion.15
  14.7 0.9 maximum_multiply_fusion.2
  15.6 0.8 fusion.160
  16.3 0.9 maximum_multiply_fusion.4
  17.2 18.2 %all-to-all-done = bf16[2,8,128,256]{3,2,0,1:T(8,128)(2,1)S(1)} async-done(((bf16[2,8,128,256]{3,2,0,1:T(8,128)(2,1)}), bf16[2,8,128,256]{3,2,0,1:T(8,128)(2,1)S(1)}, u32[]{:S(2)}, u32[]{:S(2)}) %all-to-all-start) | async-done | bytes 1048608 | tf_op jit(solution)/shard_map/all_to_all | solution.py:67
  35.5 0.8 copy-done.23
  36.4 0.7 convolution_convert_fusion.9
  37.5 0.7 convolution_convert_fusion.8
  39.4 0.7 convolution_convert_fusion.7
  40.4 0.7 convolution_convert_fusion.6
  42.3 0.7 convolution_convert_fusion.5
  43.4 0.7 convolution_convert_fusion.4
  44.5 29.3 %all_to_all.20 = bf16[2,8,128,256]{3,2,0,1:T(8,128)(2,1)S(1)} all-to-all(bf16[2,8,128,256]{3,2,0,1:T(8,128)(2,1)S(1)} %copy.56), channel_id=1, replica_groups=mesh['sx'=8,'sy'=4] {'sx'}, dimensions={1} | all-to-all | bytes 2097152 | tf_op jit(solution)/shard_map/all_to_all | solution.py:76
  73.9 1.1 copy.58
  75.0 3.5 %all-to-all-start.2 = ((bf16[2,4,256,256]{3,2,0,1:T(8,128)(2,1)}), bf16[2,4,256,256]{3,2,0,1:T(8,128)(2,1)S(1)}, u32[]{:S(2)}, u32[]{:S(2)}) async-start(bf16[2,4,256,256]{3,2,0,1:T(8,128)(2,1)} %copy.58), calls=%async_computation.2 | async-start | bytes 2097152 | tf_op jit(solution)/shard_map/all_to_all | solution.py:79
  78.5 0.8 slice_bitcast_fusion.7
  79.3 0.9 maximum_multiply_fusion.6
  80.9 12.0 %all-to-all-done.2 = bf16[2,4,256,256]{3,2,0,1:T(8,128)(2,1)S(1)} async-done(((bf16[2,4,256,256]{3,2,0,1:T(8,128)(2,1)}), bf16[2,4,256,256]{3,2,0,1:T(8,128)(2,1)S(1)}, u32[]{:S(2)}, u32[]{:S(2)}) %all-to-all-start.2) | async-done | bytes 1048608 | tf_op jit(solution)/shard_map/all_to_all | solution.py:79
  93.0 0.7 convolution_convert_fusion.3
  94.1 0.7 convolution_convert_fusion.2
  96.0 0.7 convolution_convert_fusion.1
  96.7 0.7 convolution_convert_fusion
  97.8 1.1 copy.65
  98.9 3.5 %all-to-all-start.3 = ((bf16[2,4,256,256]{3,2,0,1:T(8,128)(2,1)}), bf16[2,4,256,256]{3,2,0,1:T(8,128)(2,1)S(1)}, u32[]{:S(2)}, u32[]{:S(2)}) async-start(bf16[2,4,256,256]{3,2,0,1:T(8,128)(2,1)} %copy.65), calls=%async_computation.3 | async-start | bytes 2097152 | tf_op jit(solution)/shard_map/all_to_all | solution.py:88
  102.6 14.2 %all-to-all-done.3 = bf16[2,4,256,256]{3,2,0,1:T(8,128)(2,1)S(1)} async-done(((bf16[2,4,256,256]{3,2,0,1:T(8,128)(2,1)}), bf16[2,4,256,256]{3,2,0,1:T(8,128)(2,1)S(1)}, u32[]{:S(2)}, u32[]{:S(2)}) %all-to-all-start.3) | async-done | bytes 1048608 | tf_op jit(solution)/shard_map/all_to_all | solution.py:88
  118.3 38.6 %all_gather.3 = f32[2,4096]{1,0:T(2,128)S(1)} all-gather(f32[2,128]{1,0:T(2,128)S(1)} %pad_maximum_fusion.3), channel_id=1, replica_groups=mesh['sx'=8,'sy'=4] {'sx','sy'}, dimensions={1}, use_global_device_ids=true | all-gather | bytes 33792 | tf_op jit(solution)/shard_map/all_gather | solution.py:92
  (97 shorter events, 8.7 us)
Async XLA Ops:
  2.3 33.1 %all-to-all-start = ((bf16[2,8,128,256]{3,2,0,1:T(8,128)(2,1)}), bf16[2,8,128,256]{3,2,0,1:T(8,128)(2,1)S(1)}, u32[]{:S(2)}, u32[]{:S(2)}) async-start(bf16[2,8,128,256]{3,2,0,1:T(8,128)(2,1)} %copy.47), calls=%async_computation | async-start | bytes 2097152 | tf_op jit(solution)/shard_map/all_to_all | solution.py:67
  35.4 0.9 copy-start.23
  35.4 1.0 copy-start.24
  35.4 1.0 copy-start.25
  36.4 0.9 copy-start.5
  36.4 1.0 copy-start.6
  38.4 0.9 copy-start.11
  38.4 1.0 copy-start.12
  38.4 1.0 copy-start.22
  39.4 0.9 copy-start.3
  39.4 1.0 copy-start.4
  41.4 0.9 copy-start.10
  41.4 1.0 copy-start.21
  42.3 0.9 copy-start.1
  42.3 1.0 copy-start.2
  75.0 17.9 %all-to-all-start.2 = ((bf16[2,4,256,256]{3,2,0,1:T(8,128)(2,1)}), bf16[2,4,256,256]{3,2,0,1:T(8,128)(2,1)S(1)}, u32[]{:S(2)}, u32[]{:S(2)}) async-start(bf16[2,4,256,256]{3,2,0,1:T(8,128)(2,1)} %copy.58), calls=%async_computation.2 | async-start | bytes 2097152 | tf_op jit(solution)/shard_map/all_to_all | solution.py:79
  79.2 13.7 %copy-start.14 = (bf16[256,256]{1,0:T(8,128)(2,1)S(1)}, bf16[256,256]{1,0:T(8,128)(2,1)}, u32[]{:S(2)}) copy-start(bf16[256,256]{1,0:T(8,128)(2,1)} %get-tuple-element.96) | copy-start | bytes 393220
  79.2 13.7 %copy-start.16 = (bf16[256,256]{1,0:T(8,128)(2,1)S(1)}, bf16[256,256]{1,0:T(8,128)(2,1)}, u32[]{:S(2)}) copy-start(bf16[256,256]{1,0:T(8,128)(2,1)} %get-tuple-element.99) | copy-start | bytes 393220
  79.2 13.7 %copy-start.19 = (bf16[256,256]{1,0:T(8,128)(2,1)S(1)}, bf16[256,256]{1,0:T(8,128)(2,1)}, u32[]{:S(2)}) copy-start(bf16[256,256]{1,0:T(8,128)(2,1)} %get-tuple-element.107) | copy-start | bytes 393220
  93.0 1.0 copy-start.7
  93.0 1.0 copy-start.8
  93.0 1.0 copy-start.15
  93.0 1.1 copy-start.17
  93.0 1.1 copy-start.20
  95.0 0.9 copy-start.13
  95.1 1.0 copy-start.18
  97.8 4.6 %copy-start.9 = (f32[2,128,256]{2,1,0:T(8,128)S(1)}, f32[2,128,256]{2,1,0:T(8,128)}, u32[]{:S(2)}) copy-start(f32[2,128,256]{2,1,0:T(8,128)} %param.7) | copy-start | bytes 786436
  98.9 17.9 %all-to-all-start.3 = ((bf16[2,4,256,256]{3,2,0,1:T(8,128)(2,1)}), bf16[2,4,256,256]{3,2,0,1:T(8,128)(2,1)S(1)}, u32[]{:S(2)}, u32[]{:S(2)}) async-start(bf16[2,4,256,256]{3,2,0,1:T(8,128)(2,1)} %copy.65), calls=%async_computation.3 | async-start | bytes 2097152 | tf_op jit(solution)/shard_map/all_to_all | solution.py:88
  102.4 14.5 %copy-start = (bf16[2,128,1024]{2,1,0:T(8,128)(2,1)S(1)}, bf16[2,128,1024]{2,1,0:T(8,128)(2,1)}, u32[]{:S(2)}) copy-start(bf16[2,128,1024]{2,1,0:T(8,128)(2,1)} %param.6) | copy-start | bytes 1572868
where the time goes:
time: 158 us; the launch traced here: 157 us
  blocking collectives  67.9 us (43%)
  waiting for transfers between devices  44.3 us (28%)
  local copies, waits for them, and re-layouts  15.1 us (10%)
  starting transfers between devices  14.3 us (9%)
  matrix products  8.46 us (5%)
  other arithmetic  6.72 us (4%)
    all_gather x1, blocking collectives, local(): return lax.all_gather(closed, ('sx', 'sy'), axis=1, tiled=True)  38.6 us
    all_to_all x1, blocking collectives, local(): lax.all_to_all(grouped, 'sx', split_axis=1, concat_axis=1, tiled=True)  29.3 us
    all_to_all x1, waiting for transfers between devices, local(): lax.all_to_all(current.reshape(2, count_x, rows_dev // count_x, width), '...  18.2 us
    all_to_all x1, waiting for transfers between devices, local(): lax.all_to_all(grouped, 'sy', split_axis=1, concat_axis=1, tiled=True)  14.2 us
    all_to_all x1, waiting for transfers between devices, local(): lax.all_to_all(current.reshape(2, count_y, rows_dev // count_y, width), '...  12 us
    all_to_all x1, starting transfers between devices, local(): lax.all_to_all(current.reshape(2, count_x, rows_dev // count_x, width), '...  7.31 us
    dot_general x10, matrix products, combine(): jnp.dot(joined, matrix, preferred_element_type=jnp.float32)  7.1 us
    unnamed x59, local copies, waits for them, and re-layouts  5.51 us
  transfers between devices with their start and end apart: 3, of which 3 were waited for; matrix products, arithmetic and copies ran while one was open for 6% of the time, Pallas kernels for 0%

commit v1 on v0

v1 whole, which is shorter than its diff:
```python
import functools

import jax
import jax.numpy as jnp
from jax import lax
from jax.experimental import pallas as pl
from jax.experimental.pallas import tpu as pltpu
from jax.sharding import PartitionSpec as P

MESH = pl.DeviceIdType.MESH
CHUNKS = 8
LAG = 2


def kernel(
    plan,
    x_hbm,
    g_hbm,
    u_hbm,
    v_hbm,
    out_ref,
    xs,
    xr,
    gates,
    mix,
    back,
    ubuf,
    vraw,
    vbuf,
    wbuf,
    part,
    red,
    local_sem,
    xsend,
    xrecv,
    gsend,
    grecv,
    psend,
    precv,
):
    exchanges, gathers = plan
    rows, width2 = xs.shape[1:]
    width = width2 // 2
    slots, _, amps, _ = ubuf.shape
    step_rows = rows // CHUNKS
    coords = {"sx": lax.axis_index("sx"), "sy": lax.axis_index("sy")}

    def bit_of(axis, pos):
        return (coords[axis] // (1 << pos)) % 2

    def far(*flips):
        where = dict(coords)
        for axis, pos in flips:
            where[axis] = where[axis] + (1 << pos) * (1 - 2 * bit_of(axis, pos))
        return (where["sx"], where["sy"])

    copies = [
        pltpu.make_async_copy(x_hbm.at[0], xs.at[0, :, pl.ds(0, width)], local_sem.at[0]),
        pltpu.make_async_copy(x_hbm.at[1], xs.at[0, :, pl.ds(width, width)], local_sem.at[1]),
        pltpu.make_async_copy(v_hbm, vraw, local_sem.at[2]),
        pltpu.make_async_copy(u_hbm, ubuf.at[0], local_sem.at[3]),
        pltpu.make_async_copy(g_hbm, gates, local_sem.at[4]),
    ]
    for copy in copies:
        copy.start()

    barrier = pltpu.get_barrier_semaphore()
    peers = [(axis, pos) for axis, pos, _ in exchanges + gathers]
    for peer in peers:
        pl.semaphore_signal(barrier, inc=1, device_id=far(peer), device_id_type=MESH)
    copies[2].wait()
    vbuf[0] = vraw[...].astype(jnp.bfloat16)
    copies[0].wait()
    copies[1].wait()
    copies[3].wait()
    pl.semaphore_wait(barrier, len(peers))

    def x_copy(stage, chunk):
        here = pl.ds(chunk * step_rows, step_rows)
        return pltpu.make_async_remote_copy(
            src_ref=xs.at[stage, here],
            dst_ref=xr.at[stage, here],
            send_sem=xsend.at[stage, chunk],
            recv_sem=xrecv.at[stage, chunk],
            device_id=far(exchanges[stage][:2]),
            device_id_type=MESH,
        )

    def g_copy(step, slot, piece):
        landing = slot + (1 << step)
        if piece == 0:
            src, dst = vbuf.at[slot], vbuf.at[landing]
        else:
            src, dst = ubuf.at[slot, piece - 1], ubuf.at[landing, piece - 1]
        return pltpu.make_async_remote_copy(
            src_ref=src,
            dst_ref=dst,
            send_sem=gsend.at[landing, piece],
            recv_sem=grecv.at[landing, piece],
            device_id=far(gathers[step][:2]),
            device_id_type=MESH,
        )

    for chunk in range(CHUNKS):
        x_copy(0, chunk).start()
    for piece in range(3):
        for step in range(len(gathers)):
            g_copy(step, 0, piece).start()

    def arrive(slot, piece):
        step = slot.bit_length() - 1
        g_copy(step, slot - (1 << step), piece).wait_recv()
        for later in range(step + 1, len(gathers)):
            g_copy(later, slot, piece).start()

    copies[4].wait()
    for stage, (axis, pos, number) in enumerate(exchanges):
        sign = (1 - 2 * bit_of(axis, pos)).astype(jnp.float32).astype(jnp.bfloat16)
        for half in range(2):
            real, imag = gates[number, half, 0], gates[number, half, 1]
            if half:
                real, imag = real * sign, imag * sign
            base = half * width2
            mix[stage, pl.ds(base, width), pl.ds(0, width)] = real
            mix[stage, pl.ds(base, width), pl.ds(width, width)] = imag
            mix[stage, pl.ds(base + width, width), pl.ds(0, width)] = -imag
            mix[stage, pl.ds(base + width, width), pl.ds(width, width)] = real
    for step, (axis, pos, number) in enumerate(gathers):
        sign = (2 * bit_of(axis, pos) - 1).astype(jnp.float32).astype(jnp.bfloat16)
        for half in range(2):
            real, imag = gates[number, half, 0], gates[number, half, 1]
            if half:
                real, imag = real * sign, imag * sign
            back[step, half, pl.ds(0, width), pl.ds(0, width)] = real
            back[step, half, pl.ds(0, width), pl.ds(width, width)] = -imag
            back[step, half, pl.ds(width, width), pl.ds(0, width)] = imag
            back[step, half, pl.ds(width, width), pl.ds(width, width)] = real

    order = sorted(range(len(gathers)), key=lambda step: -gathers[step][2])

    def pull_back(slot):
        values = jnp.concatenate([vbuf[slot, 0], vbuf[slot, 1]], axis=-1)
        for place, step in enumerate(order):
            half = (slot >> step) & 1
            product = lax.dot_general(
                values,
                back[step, half],
                (((1,), (1,)), ((), ())),
                preferred_element_type=jnp.float32,
            )
            values = product.astype(jnp.bfloat16)
        wbuf[slot] = product

    def section(stage, chunk):
        x_copy(stage, chunk).wait_recv()
        here = pl.ds(chunk * step_rows, step_rows)
        joined = jnp.concatenate([xs[stage, here], xr[stage, here]], axis=-1)
        xs[stage + 1, here] = jnp.dot(
            joined, mix[stage], preferred_element_type=jnp.float32
        ).astype(jnp.bfloat16)
        if stage + 1 < len(exchanges):
            x_copy(stage + 1, chunk).start()

    todo = [(slot, piece) for piece in range(3) for slot in range(1, slots)]
    forwards = [event for event in todo if event[0] < slots // 2]
    ends = [event for event in todo if event[0] >= slots // 2]
    total = CHUNKS + LAG * (len(exchanges) - 1)
    done = 0
    pull_back(0)
    for tick in range(total):
        for stage in range(len(exchanges)):
            chunk = tick - LAG * stage
            if 0 <= chunk < CHUNKS:
                section(stage, chunk)
        until = len(forwards) * (tick + 1) // total
        for event in forwards[done:until]:
            arrive(*event)
        done = until
    for event in ends:
        if event[1] == 0:
            arrive(*event)
    for slot in range(1, slots):
        pull_back(slot)
    for event in ends:
        if event[1] > 0:
            arrive(*event)

    final = xs.at[len(exchanges)]

    def p_copy(slot):
        flips = [gathers[step][:2] for step in range(len(gathers)) if (slot >> step) & 1]
        return pltpu.make_async_remote_copy(
            src_ref=part.at[slot],
            dst_ref=red.at[slot],
            send_sem=psend.at[slot],
            recv_sem=precv.at[slot],
            device_id=far(*flips),
            device_id_type=MESH,
        )

    def fold(values):
        lanes = 128
        total_ = values[:, :lanes]
        for start in range(lanes, width, lanes):
            total_ = total_ + values[:, start : start + lanes]
        return jnp.sum(total_.T, axis=0, keepdims=True)

    for slot in reversed(range(slots)):
        by_real = jnp.dot(ubuf[slot, 0], final[...], preferred_element_type=jnp.float32)
        by_imag = jnp.dot(ubuf[slot, 1], final[...], preferred_element_type=jnp.float32)
        proj_real = by_real[:, :width] - by_imag[:, width:]
        proj_imag = by_real[:, width:] + by_imag[:, :width]
        w_real, w_imag = wbuf[slot, :, :width], wbuf[slot, :, width:]
        part[slot, 0:1] = fold(proj_real * w_real - proj_imag * w_imag)
        part[slot, 1:2] = fold(proj_real * w_imag + proj_imag * w_real)
        if slot:
            p_copy(slot).start()

    result = part[0]
    for slot in range(1, slots):
        p_copy(slot).wait_recv()
    for slot in range(1, slots):
        result = result + red[slot]
    out_ref[...] = result

    for stage in range(len(exchanges)):
        for chunk in range(CHUNKS):
            x_copy(stage, chunk).wait_send()
    for step in range(len(gathers)):
        for slot in range(1 << step):
            for piece in range(3):
                g_copy(step, slot, piece).wait_send()
    for slot in range(1, slots):
        p_copy(slot).wait_send()


def local(tensors, gates, closing_rows, closing_columns):
    current = tensors[:, 0, 0]
    rows, width = current.shape[1:]
    amps = closing_rows.shape[1]
    bits_x = lax.axis_size("sx").bit_length() - 1
    bits_y = lax.axis_size("sy").bit_length() - 1
    exchanges = [("sx", pos, pos) for pos in range(bits_x - 1)]
    gathers = [("sx", bits_x - 1, bits_x - 1)]
    gathers += [("sy", pos, bits_x + pos) for pos in reversed(range(bits_y))]
    stages, steps = len(exchanges), len(gathers)
    slots = 1 << steps
    closed = pl.pallas_call(
        functools.partial(kernel, (exchanges, gathers)),
        out_shape=jax.ShapeDtypeStruct((2, amps), jnp.float32),
        in_specs=[pl.BlockSpec(memory_space=pl.ANY)] * 4,
        out_specs=pl.BlockSpec(memory_space=pltpu.VMEM),
        scratch_shapes=[
            pltpu.VMEM((stages + 1, rows, 2 * width), jnp.bfloat16),
            pltpu.VMEM((stages, rows, 2 * width), jnp.bfloat16),
            pltpu.VMEM(gates.shape, jnp.bfloat16),
            pltpu.VMEM((stages, 4 * width, 2 * width), jnp.bfloat16),
            pltpu.VMEM((steps, 2, 2 * width, 2 * width), jnp.bfloat16),
            pltpu.VMEM((slots, 2, amps, rows), jnp.bfloat16),
            pltpu.VMEM((2, amps, width), jnp.float32),
            pltpu.VMEM((slots, 2, amps, width), jnp.bfloat16),
            pltpu.VMEM((slots, amps, 2 * width), jnp.float32),
            pltpu.VMEM((slots, 2, amps), jnp.float32),
            pltpu.VMEM((slots, 2, amps), jnp.float32),
            pltpu.SemaphoreType.DMA((5,)),
            pltpu.SemaphoreType.DMA((stages, CHUNKS)),
            pltpu.SemaphoreType.DMA((stages, CHUNKS)),
            pltpu.SemaphoreType.DMA((slots, 3)),
            pltpu.SemaphoreType.DMA((slots, 3)),
            pltpu.SemaphoreType.DMA((slots,)),
            pltpu.SemaphoreType.DMA((slots,)),
        ],
        compiler_params=pltpu.CompilerParams(
            collective_id=0, has_side_effects=True, vmem_limit_bytes=60 * 2**20
        ),
    )(current, gates, closing_rows, closing_columns)
    return lax.all_gather(closed, ("sx", "sy"), axis=1, tiled=True)


def solution(mesh):
    placed = (
        P(None, "sx", "sy", None, None),
        P(),
        P(None, ("sx", "sy"), None),
        P(None, ("sx", "sy"), None),
    )
    return jax.shard_map(local, mesh=mesh, in_specs=placed, out_specs=P(), check_vma=False)
```

time: 158 us -> 103 us (0.65)
  Pallas kernels: 0 us -> 62 us
  waiting for transfers between devices: 44.3 us -> 0 us
  blocking collectives: 67.9 us -> 40.6 us
  local copies, waits for them, and re-layouts: 15.1 us -> 0.61 us
  starting transfers between devices: 14.3 us -> 0 us
  matrix products: 8.46 us -> 0 us
  other arithmetic: 6.72 us -> 0 us
    pallas_call x0 -> x1, Pallas kernels: none -> 62 us  [local(): pl.pallas_call(functools.partial(kernel, (exchanges, gathers)), out_shape...]
    all_to_all x3 -> x0, waiting for transfers between devices: 44.3 us -> none  [the longest x1 18.2 us: local(): lax.all_to_all(current.reshape(2, count_x, rows_dev // count_x, width), '...]
    all_to_all x1 -> x0, blocking collectives: 29.3 us -> none  [local(): lax.all_to_all(grouped, 'sx', split_axis=1, concat_axis=1, tiled=True)]
    all_to_all x3 -> x0, starting transfers between devices: 14.3 us -> none  [the longest x1 7.31 us: local(): lax.all_to_all(current.reshape(2, count_x, rows_dev // count_x, width), '...]
    dot_general x14 -> x0, matrix products: 8.46 us -> none  [the longest x10 7.1 us: combine(): jnp.dot(joined, matrix, preferred_element_type=jnp.float32)]
    unnamed x59 -> x1, local copies, waits for them, and re-layouts: 5.51 us -> 0.61 us
    squeeze x4 -> x0, local copies, waits for them, and re-layouts: 4.16 us -> none  [the longest x3 2.31 us: mixing_matrix(): own_top = jnp.concatenate([gate_pair[0, 0], gate_pair[0, 1]], axis=1)]
    mul x5 -> x0, other arithmetic: 3.64 us -> none  [mixing_matrix(): far_top = jnp.concatenate([gate_pair[1, 0], gate_pair[1, 1]], axis=1) * sign]
  transfers between devices with their start and end apart: 3 -> 0, of which waited for: 3 -> 0; matrix products, arithmetic and copies ran while one was open for 6% -> 0% of each run, Pallas kernels for 0% -> 0%
where the time goes in v1:
time: 103 us
  Pallas kernels  62 us (60%)
  blocking collectives  40.6 us (39%)
    pallas_call x1, Pallas kernels, local(): pl.pallas_call(functools.partial(kernel, (exchanges, gathers)), out_shape...  62 us
    all_gather x1, blocking collectives, local(): return lax.all_gather(closed, ('sx', 'sy'), axis=1, tiled=True)  40.6 us

profile of v1, /device:TPU:0, one launch (start us, length us, event | category | flops | bytes accessed | tf_op | source)
XLA Modules:
  0.0 103.2 jit_solution(6374034179471692117)
XLA Ops:
  0.0 62.0 %shard_map.46 = f32[2,128]{1,0:T(2,128)} custom-call(bf16[2,1024,256]{2,1,0:T(8,128)(2,1)} %bitcast.1, bf16[5,2,2,256,256]{4,3,2,1,0:T(8,128)(2,1)} %g_hbm.1, bf16[2,128,1024]{2,1,0:T(8,128)(2,1)} %u_hbm.1, f32[2,128,256]{2,1,0:T(8,128)} %v_hbm.1), custom_call_target="tpu_custom_call" | custom-call | tf_op jit(solution)/shard_map/pallas_call | solution.py:248
  62.0 40.6 %all_gather.3 = f32[2,4096]{1,0:T(2,128)S(1)} all-gather(f32[2,128]{1,0:T(2,128)} %shard_map.46), channel_id=1, replica_groups=mesh['sx'=8,'sy'=4] {'sx','sy'}, dimensions={1}, use_global_device_ids=true | all-gather | bytes 33792 | tf_op jit(solution)/shard_map/all_gather | solution.py:277
  102.6 0.6 copy.6

commit v2 on v1

--- a/solution.py
+++ b/solution.py
@@ -9,7 +9,9 @@
 
 MESH = pl.DeviceIdType.MESH
 CHUNKS = 8
-LAG = 2
+LAG = 5
+HOLD = 4
+FIRST = 6
 
 
 def kernel(
@@ -28,8 +30,10 @@
     vraw,
     vbuf,
     wbuf,
+    acc,
     part,
     red,
+    every,
     local_sem,
     xsend,
     xrecv,
@@ -37,6 +41,8 @@
     grecv,
     psend,
     precv,
+    bsend,
+    brecv,
 ):
     exchanges, gathers = plan
     rows, width2 = xs.shape[1:]
@@ -72,7 +78,6 @@
     vbuf[0] = vraw[...].astype(jnp.bfloat16)
     copies[0].wait()
     copies[1].wait()
-    copies[3].wait()
     pl.semaphore_wait(barrier, len(peers))
 
     def x_copy(stage, chunk):
@@ -101,11 +106,17 @@
             device_id_type=MESH,
         )
 
+    def offer(step):
+        for piece in range(3):
+            g_copy(step, 0, piece).start()
+
     for chunk in range(CHUNKS):
         x_copy(0, chunk).start()
-    for piece in range(3):
-        for step in range(len(gathers)):
-            g_copy(step, 0, piece).start()
+    copies[3].wait()
+    early = bit_of(*gathers[0][:2]) == bit_of(*exchanges[-1][:2])
+    pl.when(early)(functools.partial(offer, 0))
+    for step in range(1, len(gathers)):
+        offer(step)
 
     def arrive(slot, piece):
         step = slot.bit_length() - 1
@@ -161,31 +172,48 @@
         if stage + 1 < len(exchanges):
             x_copy(stage + 1, chunk).start()
 
-    todo = [(slot, piece) for piece in range(3) for slot in range(1, slots)]
-    forwards = [event for event in todo if event[0] < slots // 2]
-    ends = [event for event in todo if event[0] >= slots // 2]
+    def spread(events, moments):
+        size = len(moments)
+        return {
+            moment: events[len(events) * place // size : len(events) * (place + 1) // size]
+            for place, moment in enumerate(moments)
+        }
+
     total = CHUNKS + LAG * (len(exchanges) - 1)
-    done = 0
+    wait_tick = total - CHUNKS + FIRST - 1
+    half = slots // 2
+    relays = [(slot, piece) for piece in range(3) for slot in range(2, half) if slot % 2 == 0]
+    late = [(slot, piece) for piece in range(3) for slot in range(1, half) if slot % 2]
+    late.sort(key=lambda event: (event[1] + event[0].bit_count(), event[0]))
+    ends = [(slot, piece) for piece in range(3) for slot in range(half, slots)]
+    at_tick = spread(relays, range(HOLD + 1))
+    at_tick.update(spread(late, range(HOLD + 1, wait_tick + 1)))
     pull_back(0)
+
+    def gather_rows(slot, index, start, stop):
+        return jnp.dot(
+            ubuf[slot, index, :, start:stop],
+            xs[len(exchanges), start:stop],
+            preferred_element_type=jnp.float32,
+        )
+
     for tick in range(total):
         for stage in range(len(exchanges)):
             chunk = tick - LAG * stage
             if 0 <= chunk < CHUNKS:
                 section(stage, chunk)
-        until = len(forwards) * (tick + 1) // total
-        for event in forwards[done:until]:
+        if tick == HOLD:
+            pl.when(jnp.logical_not(early))(functools.partial(offer, 0))
+        for event in at_tick.get(tick, ()):
             arrive(*event)
-        done = until
-    for event in ends:
-        if event[1] == 0:
-            arrive(*event)
-    for slot in range(1, slots):
-        pull_back(slot)
-    for event in ends:
-        if event[1] > 0:
-            arrive(*event)
-
-    final = xs.at[len(exchanges)]
+        if tick == wait_tick:
+            for event in ends:
+                arrive(*event)
+            for slot in range(1, slots):
+                pull_back(slot)
+            for slot in range(slots):
+                for index in range(2):
+                    acc[slot, index] = gather_rows(slot, index, 0, FIRST * step_rows)
 
     def p_copy(slot):
         flips = [gathers[step][:2] for step in range(len(gathers)) if (slot >> step) & 1]
@@ -206,8 +234,8 @@
         return jnp.sum(total_.T, axis=0, keepdims=True)
 
     for slot in reversed(range(slots)):
-        by_real = jnp.dot(ubuf[slot, 0], final[...], preferred_element_type=jnp.float32)
-        by_imag = jnp.dot(ubuf[slot, 1], final[...], preferred_element_type=jnp.float32)
+        by_real = acc[slot, 0] + gather_rows(slot, 0, FIRST * step_rows, rows)
+        by_imag = acc[slot, 1] + gather_rows(slot, 1, FIRST * step_rows, rows)
         proj_real = by_real[:, :width] - by_imag[:, width:]
         proj_imag = by_real[:, width:] + by_imag[:, :width]
         w_real, w_imag = wbuf[slot, :, :width], wbuf[slot, :, width:]
@@ -221,7 +249,26 @@
         p_copy(slot).wait_recv()
     for slot in range(1, slots):
         result = result + red[slot]
-    out_ref[...] = result
+    count_y = lax.axis_size("sy")
+    count = lax.axis_size("sx") * count_y
+    rank = coords["sx"] * count_y + coords["sy"]
+    every[pl.ds(rank, 1)] = result[None]
+
+    def b_copy(offset):
+        other = (rank + offset) % count
+        return pltpu.make_async_remote_copy(
+            src_ref=every.at[rank],
+            dst_ref=every.at[rank],
+            send_sem=bsend.at[offset],
+            recv_sem=brecv.at[offset],
+            device_id=(other // count_y, other % count_y),
+            device_id_type=MESH,
+        )
+
+    @pl.loop(1, count)
+    def _(offset):
+        b_copy(offset).start()
+
 
     for stage in range(len(exchanges)):
         for chunk in range(CHUNKS):
@@ -232,6 +279,13 @@
                 g_copy(step, slot, piece).wait_send()
     for slot in range(1, slots):
         p_copy(slot).wait_send()
+
+    @pl.loop(1, count)
+    def _(offset):
+        b_copy(offset).wait()
+
+    out_ref[0] = every[:, 0, :]
+    out_ref[1] = every[:, 1, :]
 
 
 def local(tensors, gates, closing_rows, closing_columns):
@@ -245,9 +299,10 @@
     gathers += [("sy", pos, bits_x + pos) for pos in reversed(range(bits_y))]
     stages, steps = len(exchanges), len(gathers)
     slots = 1 << steps
+    count = lax.axis_size("sx") * lax.axis_size("sy")
     closed = pl.pallas_call(
         functools.partial(kernel, (exchanges, gathers)),
-        out_shape=jax.ShapeDtypeStruct((2, amps), jnp.float32),
+        out_shape=jax.ShapeDtypeStruct((2, count, amps), jnp.float32),
         in_specs=[pl.BlockSpec(memory_space=pl.ANY)] * 4,
         out_specs=pl.BlockSpec(memory_space=pltpu.VMEM),
         scratch_shapes=[
@@ -260,8 +315,10 @@
             pltpu.VMEM((2, amps, width), jnp.float32),
             pltpu.VMEM((slots, 2, amps, width), jnp.bfloat16),
             pltpu.VMEM((slots, amps, 2 * width), jnp.float32),
+            pltpu.VMEM((slots, 2, amps, 2 * width), jnp.float32),
             pltpu.VMEM((slots, 2, amps), jnp.float32),
             pltpu.VMEM((slots, 2, amps), jnp.float32),
+            pltpu.VMEM((count, 2, amps), jnp.float32),
             pltpu.SemaphoreType.DMA((5,)),
             pltpu.SemaphoreType.DMA((stages, CHUNKS)),
             pltpu.SemaphoreType.DMA((stages, CHUNKS)),
@@ -269,12 +326,14 @@
             pltpu.SemaphoreType.DMA((slots, 3)),
             pltpu.SemaphoreType.DMA((slots,)),
             pltpu.SemaphoreType.DMA((slots,)),
+            pltpu.SemaphoreType.DMA((count,)),
+            pltpu.SemaphoreType.DMA((count,)),
         ],
         compiler_params=pltpu.CompilerParams(
             collective_id=0, has_side_effects=True, vmem_limit_bytes=60 * 2**20
         ),
     )(current, gates, closing_rows, closing_columns)
-    return lax.all_gather(closed, ("sx", "sy"), axis=1, tiled=True)
+    return closed.reshape(2, count * amps)
 
 
 def solution(mesh):

time: 103 us -> 64.1 us (0.62)
  blocking collectives: 40.6 us -> 0 us
    all_gather x1 -> x0, blocking collectives: 40.6 us -> none  [local(): return lax.all_gather(closed, ('sx', 'sy'), axis=1, tiled=True)]
where the time goes in v2:
time: 64.1 us; the launch traced here: 63.9 us
  Pallas kernels  62.5 us (98%)
  local copies, waits for them, and re-layouts  1.4 us (2%)
    pallas_call x1, Pallas kernels, local(): pl.pallas_call(functools.partial(kernel, (exchanges, gathers)), out_shape...  62.5 us
    unnamed x1, local copies, waits for them, and re-layouts  1.4 us

profile of v2, /device:TPU:0, one launch (start us, length us, event | category | flops | bytes accessed | tf_op | source)
XLA Modules:
  0.0 63.9 jit_solution(6427988086158312526)
XLA Ops:
  0.0 62.5 %shard_map.46 = f32[2,32,128]{2,1,0:T(8,128)} custom-call(bf16[2,1024,256]{2,1,0:T(8,128)(2,1)} %bitcast.5, bf16[5,2,2,256,256]{4,3,2,1,0:T(8,128)(2,1)} %g_hbm.1, bf16[2,128,1024]{2,1,0:T(8,128)(2,1)} %u_hbm.1, f32[2,128,256]{2,1,0:T(8,128)} %v_hbm.1), custom_call_target="tpu_custom_call" | custom-call | tf_op jit(solution)/shard_map/pallas_call | solution.py:303
  62.5 1.4 %copy.7 = f32[1,2,32,128]{3,1,2,0:T(2,128)} copy(f32[1,2,32,128]{3,2,1,0:T(8,128)} %bitcast.6) | data formatting | bytes 65536

commit v3 on v2

--- a/solution.py
+++ b/solution.py
@@ -10,7 +10,8 @@
 MESH = pl.DeviceIdType.MESH
 CHUNKS = 8
 LAG = 5
-HOLD = 4
+HOLD = 2
+VECTOR = 5
 FIRST = 6
 
 
@@ -107,14 +108,16 @@
         )
 
     def offer(step):
-        for piece in range(3):
+        for piece in range(1, 3):
             g_copy(step, 0, piece).start()
 
     for chunk in range(CHUNKS):
         x_copy(0, chunk).start()
+    for step in range(len(gathers)):
+        g_copy(step, 0, 0).start()
     copies[3].wait()
     early = bit_of(*gathers[0][:2]) == bit_of(*exchanges[-1][:2])
-    pl.when(early)(functools.partial(offer, 0))
+    offer(0)
     for step in range(1, len(gathers)):
         offer(step)
 
@@ -136,31 +139,37 @@
             mix[stage, pl.ds(base, width), pl.ds(width, width)] = imag
             mix[stage, pl.ds(base + width, width), pl.ds(0, width)] = -imag
             mix[stage, pl.ds(base + width, width), pl.ds(width, width)] = real
-    for step, (axis, pos, number) in enumerate(gathers):
-        sign = (2 * bit_of(axis, pos) - 1).astype(jnp.float32).astype(jnp.bfloat16)
-        for half in range(2):
-            real, imag = gates[number, half, 0], gates[number, half, 1]
-            if half:
-                real, imag = real * sign, imag * sign
-            back[step, half, pl.ds(0, width), pl.ds(0, width)] = real
-            back[step, half, pl.ds(0, width), pl.ds(width, width)] = -imag
-            back[step, half, pl.ds(width, width), pl.ds(0, width)] = imag
-            back[step, half, pl.ds(width, width), pl.ds(width, width)] = real
+    def build_back():
+        for step, (axis, pos, number) in enumerate(gathers):
+            sign = (2 * bit_of(axis, pos) - 1).astype(jnp.float32).astype(jnp.bfloat16)
+            for half in range(2):
+                real, imag = gates[number, half, 0], gates[number, half, 1]
+                if half:
+                    real, imag = real * sign, imag * sign
+                back[step, half, pl.ds(0, width), pl.ds(0, width)] = real
+                back[step, half, pl.ds(0, width), pl.ds(width, width)] = -imag
+                back[step, half, pl.ds(width, width), pl.ds(0, width)] = imag
+                back[step, half, pl.ds(width, width), pl.ds(width, width)] = real
 
     order = sorted(range(len(gathers)), key=lambda step: -gathers[step][2])
 
-    def pull_back(slot):
-        values = jnp.concatenate([vbuf[slot, 0], vbuf[slot, 1]], axis=-1)
+    def pull_back():
+        values = [jnp.concatenate([vbuf[slot, 0], vbuf[slot, 1]], axis=-1) for slot in range(slots)]
         for place, step in enumerate(order):
-            half = (slot >> step) & 1
-            product = lax.dot_general(
-                values,
-                back[step, half],
-                (((1,), (1,)), ((), ())),
-                preferred_element_type=jnp.float32,
-            )
-            values = product.astype(jnp.bfloat16)
-        wbuf[slot] = product
+            for half in range(2):
+                chosen = [slot for slot in range(slots) if (slot >> step) & 1 == half]
+                product = lax.dot_general(
+                    jnp.concatenate([values[slot] for slot in chosen], axis=0),
+                    back[step, half],
+                    (((1,), (1,)), ((), ())),
+                    preferred_element_type=jnp.float32,
+                )
+                for index, slot in enumerate(chosen):
+                    rows_of = product[index * amps : (index + 1) * amps]
+                    if place == len(order) - 1:
+                        wbuf[slot] = rows_of
+                    else:
+                        values[slot] = rows_of.astype(jnp.bfloat16)
 
     def section(stage, chunk):
         x_copy(stage, chunk).wait_recv()
@@ -182,20 +191,22 @@
     total = CHUNKS + LAG * (len(exchanges) - 1)
     wait_tick = total - CHUNKS + FIRST - 1
     half = slots // 2
-    relays = [(slot, piece) for piece in range(3) for slot in range(2, half) if slot % 2 == 0]
-    late = [(slot, piece) for piece in range(3) for slot in range(1, half) if slot % 2]
+    vectors = [(slot, 0) for slot in range(1, slots)]
+    relays = [(slot, piece) for piece in range(1, 3) for slot in range(2, half) if slot % 2 == 0]
+    late = [(slot, piece) for piece in range(1, 3) for slot in range(1, half) if slot % 2]
     late.sort(key=lambda event: (event[1] + event[0].bit_count(), event[0]))
-    ends = [(slot, piece) for piece in range(3) for slot in range(half, slots)]
-    at_tick = spread(relays, range(HOLD + 1))
-    at_tick.update(spread(late, range(HOLD + 1, wait_tick + 1)))
-    pull_back(0)
-
-    def gather_rows(slot, index, start, stop):
+    ends = [(slot, piece) for piece in range(1, 3) for slot in range(half, slots)]
+    at_tick = spread(vectors, range(VECTOR))
+    for events in (spread(relays, range(1, HOLD + 1)), spread(late, range(HOLD + 1, wait_tick + 1))):
+        for moment in events:
+            at_tick[moment] = at_tick.get(moment, []) + events[moment]
+
+    def gather_rows(start, stop):
         return jnp.dot(
-            ubuf[slot, index, :, start:stop],
+            ubuf[:, :, :, start:stop].reshape(slots * 2 * amps, stop - start),
             xs[len(exchanges), start:stop],
             preferred_element_type=jnp.float32,
-        )
+        ).reshape(slots, 2, amps, 2 * width)
 
     for tick in range(total):
         for stage in range(len(exchanges)):
@@ -203,17 +214,17 @@
             if 0 <= chunk < CHUNKS:
                 section(stage, chunk)
         if tick == HOLD:
-            pl.when(jnp.logical_not(early))(functools.partial(offer, 0))
+            pass
         for event in at_tick.get(tick, ()):
             arrive(*event)
+        if tick == VECTOR - 1:
+            build_back()
+        if tick == VECTOR:
+            pull_back()
         if tick == wait_tick:
             for event in ends:
                 arrive(*event)
-            for slot in range(1, slots):
-                pull_back(slot)
-            for slot in range(slots):
-                for index in range(2):
-                    acc[slot, index] = gather_rows(slot, index, 0, FIRST * step_rows)
+            acc[...] = gather_rows(0, FIRST * step_rows)
 
     def p_copy(slot):
         flips = [gathers[step][:2] for step in range(len(gathers)) if (slot >> step) & 1]
@@ -233,9 +244,9 @@
             total_ = total_ + values[:, start : start + lanes]
         return jnp.sum(total_.T, axis=0, keepdims=True)
 
+    acc[...] += gather_rows(FIRST * step_rows, rows)
     for slot in reversed(range(slots)):
-        by_real = acc[slot, 0] + gather_rows(slot, 0, FIRST * step_rows, rows)
-        by_imag = acc[slot, 1] + gather_rows(slot, 1, FIRST * step_rows, rows)
+        by_real, by_imag = acc[slot, 0], acc[slot, 1]
         proj_real = by_real[:, :width] - by_imag[:, width:]
         proj_imag = by_real[:, width:] + by_imag[:, :width]
         w_real, w_imag = wbuf[slot, :, :width], wbuf[slot, :, width:]

time: 64.1 us -> 61.9 us (0.966)
  Pallas kernels: 62.5 us -> 60.3 us
    pallas_call x1, Pallas kernels: 62.5 us -> 60.3 us  [local(): pl.pallas_call(functools.partial(kernel, (exchanges, gathers)), out_shape...]
where the time goes in v3:
time: 61.9 us; the launch traced here: 61.7 us
  Pallas kernels  60.3 us (97%)
  local copies, waits for them, and re-layouts  1.4 us (2%)
    pallas_call x1, Pallas kernels, local(): pl.pallas_call(functools.partial(kernel, (exchanges, gathers)), out_shape...  60.3 us
    unnamed x1, local copies, waits for them, and re-layouts  1.4 us

profile of v3, /device:TPU:0, one launch (start us, length us, event | category | flops | bytes accessed | tf_op | source)
XLA Modules:
  0.0 61.7 jit_solution(17593674671958650606)
XLA Ops:
  0.0 60.3 %shard_map.46 = f32[2,32,128]{2,1,0:T(8,128)} custom-call(bf16[2,1024,256]{2,1,0:T(8,128)(2,1)} %bitcast.5, bf16[5,2,2,256,256]{4,3,2,1,0:T(8,128)(2,1)} %g_hbm.1, bf16[2,128,1024]{2,1,0:T(8,128)(2,1)} %u_hbm.1, f32[2,128,256]{2,1,0:T(8,128)} %v_hbm.1), custom_call_target="tpu_custom_call" | custom-call | tf_op jit(solution)/shard_map/pallas_call | solution.py:314
  60.3 1.4 %copy.7 = f32[1,2,32,128]{3,1,2,0:T(2,128)} copy(f32[1,2,32,128]{3,2,1,0:T(8,128)} %bitcast.6) | data formatting | bytes 65536

commit v4 on v3

--- a/solution.py
+++ b/solution.py
@@ -12,6 +12,7 @@
 LAG = 5
 HOLD = 2
 VECTOR = 5
+PARTS = 4
 FIRST = 6
 
 
@@ -97,7 +98,8 @@
         if piece == 0:
             src, dst = vbuf.at[slot], vbuf.at[landing]
         else:
-            src, dst = ubuf.at[slot, piece - 1], ubuf.at[landing, piece - 1]
+            span = pl.ds((piece - 1) * (rows // PARTS), rows // PARTS)
+            src, dst = ubuf.at[slot, :, :, span], ubuf.at[landing, :, :, span]
         return pltpu.make_async_remote_copy(
             src_ref=src,
             dst_ref=dst,
@@ -108,7 +110,7 @@
         )
 
     def offer(step):
-        for piece in range(1, 3):
+        for piece in range(1, PARTS + 1):
             g_copy(step, 0, piece).start()
 
     for chunk in range(CHUNKS):
@@ -192,10 +194,12 @@
     wait_tick = total - CHUNKS + FIRST - 1
     half = slots // 2
     vectors = [(slot, 0) for slot in range(1, slots)]
-    relays = [(slot, piece) for piece in range(1, 3) for slot in range(2, half) if slot % 2 == 0]
-    late = [(slot, piece) for piece in range(1, 3) for slot in range(1, half) if slot % 2]
+    relays = [(slot, piece) for piece in range(1, PARTS + 1) for slot in range(2, half) if slot % 2 == 0]
+    late = [(slot, piece) for piece in range(1, PARTS + 1) for slot in range(1, half) if slot % 2]
     late.sort(key=lambda event: (event[1] + event[0].bit_count(), event[0]))
-    ends = [(slot, piece) for piece in range(1, 3) for slot in range(half, slots)]
+    tail = [event for event in late if event[1] == PARTS and event[0].bit_count() > 1]
+    late = [event for event in late if event not in tail]
+    ends = [(slot, piece) for piece in range(1, PARTS + 1) for slot in range(half, slots)]
     at_tick = spread(vectors, range(VECTOR))
     for events in (spread(relays, range(1, HOLD + 1)), spread(late, range(HOLD + 1, wait_tick + 1))):
         for moment in events:
@@ -223,8 +227,12 @@
             pull_back()
         if tick == wait_tick:
             for event in ends:
-                arrive(*event)
+                if event[1] < PARTS:
+                    arrive(*event)
             acc[...] = gather_rows(0, FIRST * step_rows)
+            for event in tail + ends:
+                if event[1] == PARTS:
+                    arrive(*event)
 
     def p_copy(slot):
         flips = [gathers[step][:2] for step in range(len(gathers)) if (slot >> step) & 1]
@@ -286,7 +294,7 @@
             x_copy(stage, chunk).wait_send()
     for step in range(len(gathers)):
         for slot in range(1 << step):
-            for piece in range(3):
+            for piece in range(PARTS + 1):
                 g_copy(step, slot, piece).wait_send()
     for slot in range(1, slots):
         p_copy(slot).wait_send()
@@ -333,8 +341,8 @@
             pltpu.SemaphoreType.DMA((5,)),
             pltpu.SemaphoreType.DMA((stages, CHUNKS)),
             pltpu.SemaphoreType.DMA((stages, CHUNKS)),
-            pltpu.SemaphoreType.DMA((slots, 3)),
-            pltpu.SemaphoreType.DMA((slots, 3)),
+            pltpu.SemaphoreType.DMA((slots, PARTS + 1)),
+            pltpu.SemaphoreType.DMA((slots, PARTS + 1)),
             pltpu.SemaphoreType.DMA((slots,)),
             pltpu.SemaphoreType.DMA((slots,)),
             pltpu.SemaphoreType.DMA((count,)),

time: 61.9 us -> 62.1 us (level)
  no operation moved by 1% of the time
where the time goes in v4:
time: 62.1 us; the launch traced here: 62 us
  Pallas kernels  60.6 us (98%)
  local copies, waits for them, and re-layouts  1.4 us (2%)
    pallas_call x1, Pallas kernels, local(): pl.pallas_call(functools.partial(kernel, (exchanges, gathers)), out_shape...  60.6 us
    unnamed x1, local copies, waits for them, and re-layouts  1.4 us

profile of v4, /device:TPU:0, one launch (start us, length us, event | category | flops | bytes accessed | tf_op | source)
XLA Modules:
  0.0 62.0 jit_solution(9160181209052689039)
XLA Ops:
  0.0 60.6 %shard_map.46 = f32[2,32,128]{2,1,0:T(8,128)} custom-call(bf16[2,1024,256]{2,1,0:T(8,128)(2,1)} %bitcast.5, bf16[5,2,2,256,256]{4,3,2,1,0:T(8,128)(2,1)} %g_hbm.1, bf16[2,128,1024]{2,1,0:T(8,128)(2,1)} %u_hbm.1, f32[2,128,256]{2,1,0:T(8,128)} %v_hbm.1), custom_call_target="tpu_custom_call" | custom-call | tf_op jit(solution)/shard_map/pallas_call | solution.py:322
  60.6 1.4 %copy.7 = f32[1,2,32,128]{3,1,2,0:T(2,128)} copy(f32[1,2,32,128]{3,2,1,0:T(8,128)} %bitcast.6) | data formatting | bytes 65536
